TPU v7x, 32 devices: a whole 2x2x4 slice. The times are simulated.
32 devices in a mesh: gx: 4 (over y, core), gy: 2 (over x), gz: 4 (over z).
Axes of the slice: x: 2, y: 2, z: 4, core: 2. Of those that a mesh axis runs over, the one named last changes fastest.
Arguments:
- old_basis: float32 [4, 32, 32, 512], P(None, 'gx', 'gy', 'gz'), may hold values from -4 to 4, as said below
- previous: float32 [4, 32, 32, 512], P(None, 'gx', 'gy', 'gz'), as said below
- incoming: float32 [4, 32, 32, 512], P(None, 'gx', 'gy', 'gz'), may hold values from -6 to 6
- coefficient: float32 [32, 32, 512], P('gx', 'gy', 'gz'), may hold values from 0.5 to 4
Outputs:
- orthonormal: float32 [4, 32, 32, 512], P(None, 'gx', 'gy', 'gz')
- projection: float32 [4, 4], replicated
- triangle: float32 [4, 4], replicated
- preconditioned: float32 [4, 32, 32, 512], P(None, 'gx', 'gy', 'gz')
- operated: float32 [4, 32, 32, 512], P(None, 'gx', 'gy', 'gz')
Inputs may be any that keep to these rules, and one draw needn't show every extreme that they name: `old_basis`: entries of order one; the basis vectors are independent, so every Gram matrix formed from them is well conditioned. `previous`: entries of order one; each vector has a part outside the span of old_basis of norm of order one under the inner product.
All inputs are finite; a program needn't handle non-finite values.
Results may differ from a plain program's by a relative error of at most 0.0003.
Values sent between devices are 32-bit elements; how exact they have to be, the bound alone decides.
No kernel may reach another device: no remote copies, remote signals or barrier semaphores. Data moves between devices by JAX's collectives and lax.ppermute only.
A program may use at most 64 MiB of HBM per device.

v0:
```python
import jax
import jax.numpy as jnp
from jax import lax
from jax.sharding import PartitionSpec as P

LEVELS = 6
COARSE_SWEEPS = 4
OMEGA = 0.8
HIGH = lax.Precision.HIGHEST


def with_halo(shard, sides, width):
    for axis, dim in sides:
        count, length = (lax.axis_size(axis), shard.shape[dim])
        up = [(i, (i + 1) % count) for i in range(count - 1)]
        down = [(j, i) for i, j in up]
        last = lax.slice_in_dim(shard, length - width, length, axis=dim)
        leading = lax.slice_in_dim(shard, 0, width, axis=dim)
        before = lax.ppermute(last, axis, up)
        after = lax.ppermute(leading, axis, down)
        shard = jnp.concatenate([before, shard, after], axis=dim)
    return shard


def stencil(extended, coeffs, factor):
    center = extended[:, 1:-1, 1:-1, 1:-1]
    total = extended[:, 2:, 1:-1, 1:-1] + extended[:, :-2, 1:-1, 1:-1]
    total = total + extended[:, 1:-1, 2:, 1:-1] + extended[:, 1:-1, :-2, 1:-1]
    total = total + extended[:, 1:-1, 1:-1, 2:] + extended[:, 1:-1, 1:-1, :-2]
    return factor * coeffs * (6.0 * center - total)


def zero_margin(field):
    return jnp.pad(field, ((0, 0), (1, 1), (1, 1), (1, 1)))


def with_faces(field):
    return with_halo(field, (("gx", 1), ("gy", 2), ("gz", 3)), 1)


def restrict(field):
    depth, size_a, size_b, size_c = field.shape
    return field.reshape(depth, size_a // 2, 2, size_b // 2, 2, size_c // 2, 2).mean(axis=(2, 4, 6))


def prolong(field):
    return jnp.repeat(jnp.repeat(jnp.repeat(field, 2, axis=1), 2, axis=2), 2, axis=3)


def whole_cycle(source, coeff_list, level):
    coeffs = coeff_list[level]
    factor = 0.25**level
    diagonal = 6.0 * factor * coeffs
    iterate = OMEGA * source / diagonal
    if level == LEVELS - 1:
        for sweep in range(COARSE_SWEEPS - 1):
            iterate = (
                iterate
                + OMEGA * (source - stencil(zero_margin(iterate), coeffs, factor)) / diagonal
            )
        return iterate
    iterate = iterate + OMEGA * (source - stencil(zero_margin(iterate), coeffs, factor)) / diagonal
    residue = source - stencil(zero_margin(iterate), coeffs, factor)
    iterate = iterate + prolong(whole_cycle(restrict(residue), coeff_list, level + 1))
    iterate = iterate + OMEGA * (source - stencil(zero_margin(iterate), coeffs, factor)) / diagonal
    return iterate


def agglomerate(source, coeffs, start_level):
    vectors = source.shape[0]
    stacked = jnp.concatenate([source, coeffs[None]], axis=0)
    depth, size_a, size_b, size_c = stacked.shape
    flattened = stacked.reshape(depth, size_a * size_b * size_c)
    gathered = lax.all_gather(flattened, ("gx", "gy", "gz"), axis=1, tiled=True)
    count_x, count_y, count_z = (lax.axis_size("gx"), lax.axis_size("gy"), lax.axis_size("gz"))
    gathered = gathered.reshape(depth, count_x, count_y, count_z, size_a, size_b, size_c)
    gathered = gathered.transpose(0, 1, 4, 2, 5, 3, 6).reshape(
        depth, count_x * size_a, count_y * size_b, count_z * size_c
    )
    coarse_list = [gathered[vectors]]
    for level in range(LEVELS - 1 - start_level):
        coarse_list.append(restrict(coarse_list[-1][None])[0])
    solution = whole_cycle(gathered[:vectors], [None] * start_level + coarse_list, start_level)
    starts = (
        jnp.zeros((), jnp.int32),
        lax.axis_index("gx") * size_a,
        lax.axis_index("gy") * size_b,
        lax.axis_index("gz") * size_c,
    )
    return lax.dynamic_slice(solution, starts, (vectors, size_a, size_b, size_c))


def local_cycle(source, coeff_list, level, start_level):
    coeffs = coeff_list[level]
    if level == start_level:
        return agglomerate(source, coeffs, start_level)
    factor = 0.25**level
    diagonal = 6.0 * factor * coeffs
    vectors = source.shape[0]
    stacked = jnp.concatenate([source, coeffs[None]], axis=0)
    widened = with_halo(stacked, (("gx", 1), ("gy", 2), ("gz", 3)), 2)
    source_wide = widened[:vectors]
    coeff_wide = widened[vectors]
    safe_wide = jnp.where(coeff_wide > 0.0, coeff_wide, 1.0)
    sweep_one = OMEGA * source_wide / (6.0 * factor * safe_wide)
    inner_coeff = coeff_wide[1:-1, 1:-1, 1:-1]
    inner_safe = safe_wide[1:-1, 1:-1, 1:-1]
    sweep_two = sweep_one[:, 1:-1, 1:-1, 1:-1] + OMEGA * (
        source_wide[:, 1:-1, 1:-1, 1:-1] - stencil(sweep_one, inner_coeff, factor)
    ) / (6.0 * factor * inner_safe)
    iterate = sweep_two[:, 1:-1, 1:-1, 1:-1]
    residue = source - stencil(sweep_two, coeffs, factor)
    iterate = iterate + prolong(local_cycle(restrict(residue), coeff_list, level + 1, start_level))
    iterate = iterate + OMEGA * (source - stencil(with_faces(iterate), coeffs, factor)) / diagonal
    return iterate


def triangular_inverse(lower):
    order = lower.shape[0]
    identity = jnp.eye(order, dtype=lower.dtype)
    inverse = jnp.zeros_like(lower)
    for row in range(order):
        values = identity[row] - jnp.dot(lower[row, :row], inverse[:row], precision=HIGH)
        inverse = inverse.at[row].set(values / lower[row, row])
    return inverse


def per_device(old_basis, previous, incoming, coefficient):
    local_cells = old_basis.shape[1] * old_basis.shape[2] * old_basis.shape[3]
    total_cells = float(
        local_cells * lax.axis_size("gx") * lax.axis_size("gy") * lax.axis_size("gz")
    )
    basis_local = jnp.einsum("mxyz,jxyz->mj", old_basis, previous, precision=HIGH)
    projection = lax.psum(basis_local, ("gx", "gy", "gz")) / total_cells
    remainder = previous - jnp.einsum("mxyz,mj->jxyz", old_basis, projection, precision=HIGH)
    gram_local = jnp.einsum("ixyz,jxyz->ij", remainder, remainder, precision=HIGH)
    gram = lax.psum(gram_local, ("gx", "gy", "gz")) / total_cells
    start_level = LEVELS - 3
    coeff_list = [coefficient]
    for level in range(start_level):
        coeff_list.append(restrict(coeff_list[-1][None])[0])
    preconditioned = local_cycle(incoming, coeff_list, 0, start_level)
    operated = stencil(with_faces(preconditioned), coefficient, 1.0)
    lower = jnp.linalg.cholesky(gram)
    inverse = triangular_inverse(lower)
    orthonormal = jnp.einsum("ji,ixyz->jxyz", inverse, remainder, precision=HIGH)
    return (orthonormal, projection, lower.T, preconditioned, operated)


def solution(mesh):
    in_specs = (
        P(None, "gx", "gy", "gz"),
        P(None, "gx", "gy", "gz"),
        P(None, "gx", "gy", "gz"),
        P("gx", "gy", "gz"),
    )
    out_specs = (
        P(None, "gx", "gy", "gz"),
        P(),
        P(),
        P(None, "gx", "gy", "gz"),
        P(None, "gx", "gy", "gz"),
    )
    return jax.shard_map(
        per_device, mesh=mesh, in_specs=in_specs, out_specs=out_specs, check_vma=False
    )
```

profile of v0, /device:TPU:25, one launch (start us, length us, event | category | flops | bytes accessed | tf_op | source)
XLA Modules:
  0.0 369.9 jit_solution(2257460580880497571)
XLA Ops:
  1.6 3.7 %collective-permute-start = (f32[5,2,16,128]{3,2,1,0:T(8,128)S(1)}, f32[5,2,16,128]{3,2,1,0:T(8,128)S(1)}, u32[]{:S(2)}, u32[]{:S(2)}) collective-permute-start(f32[5,2,16,128]{3,2,1,0:T(8,128)S(1)} %get-tuple-element.122), channel_id=1, source_target_pairs={{0,8},{8,16},{16,24},{1,9},{9,17},{17,25},{2,10},{10,18},{18,26},{... | collective-permute-start | bytes 245768 | tf_op jit(solution)/shard_map/ppermute | solution.py:19
  5.3 1.9 collective-permute-start.1
  7.3 3.8 %collective-permute-done.1 = f32[5,2,16,128]{3,2,1,0:T(8,128)S(1)} collective-permute-done((f32[5,2,16,128]{3,2,1,0:T(8,128)S(1)}, f32[5,2,16,128]{3,2,1,0:T(8,128)S(1)}, u32[]{:S(2)}, u32[]{:S(2)}) %collective-permute-start.1) | collective-permute-done | bytes 81952 | tf_op jit(solution)/shard_map/ppermute | solution.py:20
  12.1 3.1 collective-permute-start.2
  15.3 1.3 collective-permute-start.3
  16.6 2.4 convolution_bitcast_fusion.1
  19.0 5.5 %reshape_broadcast_in_dim.3 = f32[4,2,8,2,64,2]{5,4,3,2,1,0:T(8,128)} reshape(f32[8,16,128]{2,1,0:T(8,128)S(1)} %copy-done.1) | data formatting | bytes 131072 | tf_op jit(solution)/shard_map/reshape;broadcast_in_dim | solution.py:43
  24.5 2.6 reduce_sum.103
  29.8 4.0 %collective-permute-start.5 = (f32[5,12,20,2]{2,3,1,0:T(2,128)S(1)}, f32[5,12,20,2]{2,3,1,0:T(2,128)S(1)}, u32[]{:S(2)}, u32[]{:S(2)}) collective-permute-start(f32[5,12,20,2]{2,3,1,0:T(2,128)S(1)} %copy.767), channel_id=1, source_target_pairs={{1,0},{2,1},{3,2},{5,4},{6,5},{7,6},{9,8},{10,9},{11,10},{13,12},{... | collective-permute-start | bytes 28808 | tf_op jit(solution)/shard_map/ppermute | solution.py:20
  33.8 38.6 %psum.14 = f32[4,4]{0,1:T(4,128)S(1)} all-reduce(f32[4,4]{0,1:T(4,128)S(1)} %convolution_bitcast_fusion.1), channel_id=1, replica_groups=mesh['gx'=4,'gy'=2,'gz'=4] {'gx','gy','gz'}, use_global_device_ids=true, to_apply=%region_0.0 | all-reduce | flops 16 | bytes 128 | tf_op jit(solution)/shard_map/psum | solution.py:134
  74.6 1.9 fusion.12
  77.0 4.7 %copy.690 = f32[4,8,16,128]{0,3,2,1:T(8,128)} copy(f32[4,8,16,128]{3,2,1,0:T(8,128)S(1)} %fusion.35) | data formatting | bytes 524288 | tf_op jit(solution)/shard_map/sub | solution.py:112
  81.7 8.7 %reduce_sum.102 = f32[4,4,8,64]{0,3,2,1:T(8,128)S(1)} reduce(f32[4,4,2,8,2,64,2]{0,6,5,4,3,2,1:T(2,128)} %bitcast.130, f32[]{:T(128)} %constant.248.clone.1), dimensions={2,4,6}, to_apply=%region_4.0 | reduce | flops 57344 | bytes 294916 | tf_op jit(solution)/shard_map/reduce_sum | solution.py:43
  90.8 5.3 %collective-permute-start.6 = (f32[5,2,8,64]{3,2,1,0:T(8,128)S(1)}, f32[5,2,8,64]{3,2,1,0:T(8,128)S(1)}, u32[]{:S(2)}, u32[]{:S(2)}) collective-permute-start(f32[5,2,8,64]{3,2,1,0:T(8,128)S(1)} %get-tuple-element.154), channel_id=1, source_target_pairs={{0,8},{8,16},{16,24},{1,9},{9,17},{17,25},{2,10},{10,18},{18,26},{... | collective-permute-start | bytes 61448 | tf_op jit(solution)/shard_map/ppermute | solution.py:19
  96.1 2.1 collective-permute-start.7
  99.7 1.7 collective-permute-done.7
  101.5 1.8 collective-permute-start.8
  103.2 1.3 collective-permute-start.9
  104.6 3.4 collective-permute-done.9
  108.1 1.3 collective-permute-start.10
  109.4 4.0 %collective-permute-start.11 = (f32[5,8,12,2]{3,1,2,0:T(8,128)S(1)}, f32[5,8,12,2]{3,1,2,0:T(8,128)S(1)}, u32[]{:S(2)}, u32[]{:S(2)}) collective-permute-start(f32[5,8,12,2]{3,1,2,0:T(8,128)S(1)} %get-tuple-element.131), channel_id=1, source_target_pairs={{1,0},{2,1},{3,2},{5,4},{6,5},{7,6},{9,8},{10,9},{11,10},{13,12},{... | collective-permute-start | bytes 11528 | tf_op jit(solution)/shard_map/ppermute | solution.py:20
  114.7 2.7 collective-permute-done.10
  117.4 1.8 collective-permute-done.11
  121.7 1.9 collective-permute-start.12
  123.6 2.4 collective-permute-start.13
  126.0 38.6 %psum.15 = f32[4,4]{0,1:T(4,128)S(1)} all-reduce(f32[4,4]{0,1:T(4,128)S(1)} %convolution_bitcast_fusion), channel_id=1, replica_groups=mesh['gx'=4,'gy'=2,'gz'=4] {'gx','gy','gz'}, use_global_device_ids=true, to_apply=%region_1.0 | all-reduce | flops 16 | bytes 128 | tf_op jit(solution)/shard_map/psum | solution.py:137
  164.7 4.3 %collective-permute-start.14 = (f32[5,6,2,32]{3,2,1,0:T(2,128)S(1)}, f32[5,6,2,32]{3,2,1,0:T(2,128)S(1)}, u32[]{:S(2)}, u32[]{:S(2)}) collective-permute-start(f32[5,6,2,32]{3,2,1,0:T(2,128)S(1)} %get-tuple-element.158), channel_id=1, source_target_pairs={{0,4},{1,5},{2,6},{3,7},{8,12},{9,13},{10,14},{11,15},{16,20},{17,... | collective-permute-start | bytes 23048 | tf_op jit(solution)/shard_map/ppermute | solution.py:19
  169.0 1.3 collective-permute-start.15
  170.5 3.1 collective-permute-done.15
  173.8 1.3 collective-permute-start.16
  175.1 4.0 %collective-permute-start.17 = (f32[5,6,8,2]{3,2,1,0:T(8,128)S(1)}, f32[5,6,8,2]{3,2,1,0:T(8,128)S(1)}, u32[]{:S(2)}, u32[]{:S(2)}) collective-permute-start(f32[5,6,8,2]{3,2,1,0:T(8,128)S(1)} %get-tuple-element.151), channel_id=1, source_target_pairs={{1,0},{2,1},{3,2},{5,4},{6,5},{7,6},{9,8},{10,9},{11,10},{13,12},{... | collective-permute-start | bytes 5768 | tf_op jit(solution)/shard_map/ppermute | solution.py:20
  179.4 1.5 collective-permute-done.17
  181.9 61.1 %all-gather = f32[32,32,5]{1,2,0:T(8,128)S(1)} all-gather(f32[1,32,5]{1,2,0:T(8,128)S(1)} %maximum_bitcast_fusion), channel_id=1, replica_groups=mesh['gx'=4,'gy'=2,'gz'=4] {'gx','gy','gz'}, dimensions={0}, use_global_device_ids=true | all-gather | bytes 21120 | tf_op jit(solution)/shard_map/all_gather | solution.py:74
  247.3 8.6 %collective-permute-start.18 = (f32[4,1,4,32]{3,2,1,0:T(4,128)S(1)}, f32[4,1,4,32]{3,2,1,0:T(4,128)S(1)}, u32[]{:S(2)}, u32[]{:S(2)}) collective-permute-start(f32[4,1,4,32]{3,2,1,0:T(4,128)S(1)} %get-tuple-element.175), channel_id=1, source_target_pairs={{8,0},{16,8},{24,16},{9,1},{17,9},{25,17},{10,2},{18,10},{26,18},{... | collective-permute-start | bytes 6152 | tf_op jit(solution)/shard_map/ppermute | solution.py:20
  256.0 3.6 collective-permute-start.19
  260.3 3.2 collective-permute-start.21
  264.9 3.0 collective-permute-done.20
  268.1 1.7 collective-permute-start.22
  271.7 4.3 %collective-permute-done.23 = f32[4,4,6,1]{3,1,2,0:T(4,128)S(1)} collective-permute-done((f32[4,4,6,1]{3,1,2,0:T(4,128)S(1)}, f32[4,4,6,1]{3,1,2,0:T(4,128)S(1)}, u32[]{:S(2)}, u32[]{:S(2)}) %collective-permute-start.23) | collective-permute-done | bytes 416 | tf_op jit(solution)/shard_map/ppermute | solution.py:19
  276.8 2.8 collective-permute-start.24
  279.6 5.3 %collective-permute-start.25 = (f32[4,1,8,64]{3,2,1,0:T(8,128)S(1)}, f32[4,1,8,64]{3,2,1,0:T(8,128)S(1)}, u32[]{:S(2)}, u32[]{:S(2)}) collective-permute-start(f32[4,1,8,64]{3,2,1,0:T(8,128)S(1)} %get-tuple-element.156), channel_id=1, source_target_pairs={{0,8},{8,16},{16,24},{1,9},{9,17},{17,25},{2,10},{10,18},{18,26},{... | collective-permute-start | bytes 24584 | tf_op jit(solution)/shard_map/ppermute | solution.py:19
  285.8 1.4 collective-permute-start.27
  289.2 3.1 collective-permute-done.26
  292.4 3.7 %collective-permute-start.28 = (f32[4,6,10,1]{3,0,2,1:T(4,128)S(1)}, f32[4,6,10,1]{3,0,2,1:T(4,128)S(1)}, u32[]{:S(2)}, u32[]{:S(2)}) collective-permute-start(f32[4,6,10,1]{3,0,2,1:T(4,128)S(1)} %get-tuple-element.146), channel_id=1, source_target_pairs={{1,0},{2,1},{3,2},{5,4},{6,5},{7,6},{9,8},{10,9},{11,10},{13,12},{... | collective-permute-start | bytes 2888 | tf_op jit(solution)/shard_map/ppermute | solution.py:20
  298.2 4.1 %collective-permute-done.29 = f32[4,6,10,1]{3,0,2,1:T(4,128)S(1)} collective-permute-done((f32[4,6,10,1]{3,0,2,1:T(4,128)S(1)}, f32[4,6,10,1]{3,0,2,1:T(4,128)S(1)}, u32[]{:S(2)}, u32[]{:S(2)}) %collective-permute-start.29) | collective-permute-done | bytes 992 | tf_op jit(solution)/shard_map/ppermute | solution.py:19
  302.7 1.4 copy.740
  304.0 1.4 broadcast_in_dim.131
  305.4 1.3 copy.741
  307.8 1.9 collective-permute-start.30
  309.8 6.7 %collective-permute-start.31 = (f32[4,1,16,128]{3,2,1,0:T(8,128)S(1)}, f32[4,1,16,128]{3,2,1,0:T(8,128)S(1)}, u32[]{:S(2)}, u32[]{:S(2)}) collective-permute-start(f32[4,1,16,128]{3,2,1,0:T(8,128)S(1)} %get-tuple-element.128), channel_id=1, source_target_pairs={{0,8},{8,16},{16,24},{1,9},{9,17},{17,25},{2,10},{10,18},{18,26},{... | collective-permute-start | bytes 98312 | tf_op jit(solution)/shard_map/ppermute | solution.py:19
  316.5 1.9 subtract_divide_fusion
  318.5 1.4 collective-permute-start.33
  322.3 3.0 collective-permute-done.32
  325.5 3.7 collective-permute-start.34
  329.2 1.3 collective-permute-start.35
  331.4 4.0 %collective-permute-done.34 = f32[4,10,18,1]{3,0,2,1:T(4,128)S(1)} collective-permute-done((f32[4,10,18,1]{3,0,2,1:T(4,128)S(1)}, f32[4,10,18,1]{3,0,2,1:T(4,128)S(1)}, u32[]{:S(2)}, u32[]{:S(2)}) %collective-permute-start.34) | collective-permute-done | bytes 2912 | tf_op jit(solution)/shard_map/ppermute | solution.py:20
  335.4 4.1 %collective-permute-done.35 = f32[4,10,18,1]{3,0,2,1:T(4,128)S(1)} collective-permute-done((f32[4,10,18,1]{3,0,2,1:T(4,128)S(1)}, f32[4,10,18,1]{3,0,2,1:T(4,128)S(1)}, u32[]{:S(2)}, u32[]{:S(2)}) %collective-permute-start.35) | collective-permute-done | bytes 2912 | tf_op jit(solution)/shard_map/ppermute | solution.py:19
  340.2 1.9 collective-permute-start.36
  342.1 4.1 %collective-permute-start.37 = (f32[4,1,16,128]{3,2,1,0:T(8,128)S(1)}, f32[4,1,16,128]{3,2,1,0:T(8,128)S(1)}, u32[]{:S(2)}, u32[]{:S(2)}) collective-permute-start(f32[4,1,16,128]{3,2,1,0:T(8,128)S(1)} %get-tuple-element.126), channel_id=1, source_target_pairs={{0,8},{8,16},{16,24},{1,9},{9,17},{17,25},{2,10},{10,18},{18,26},{... | collective-permute-start | bytes 98312 | tf_op jit(solution)/shard_map/ppermute | solution.py:19
  347.3 1.4 collective-permute-start.39
  350.9 3.0 collective-permute-done.38
  354.2 1.9 collective-permute-start.40
  359.5 4.7 %collective-permute-done.40 = f32[4,10,18,1]{3,0,2,1:T(4,128)S(1)} collective-permute-done((f32[4,10,18,1]{3,0,2,1:T(4,128)S(1)}, f32[4,10,18,1]{3,0,2,1:T(4,128)S(1)}, u32[]{:S(2)}, u32[]{:S(2)}) %collective-permute-start.40) | collective-permute-done | bytes 2912 | tf_op jit(solution)/shard_map/ppermute | solution.py:20
  364.2 4.4 %collective-permute-done.41 = f32[4,10,18,1]{3,0,2,1:T(4,128)S(1)} collective-permute-done((f32[4,10,18,1]{3,0,2,1:T(4,128)S(1)}, f32[4,10,18,1]{3,0,2,1:T(4,128)S(1)}, u32[]{:S(2)}, u32[]{:S(2)}) %collective-permute-start.41) | collective-permute-done | bytes 2912 | tf_op jit(solution)/shard_map/ppermute | solution.py:19
  (239 shorter events, 42.6 us)
Async XLA Ops:
  0.6 18.4 %copy-start.1 = (f32[8,16,128]{2,1,0:T(8,128)S(1)}, f32[8,16,128]{2,1,0:T(8,128)}, u32[]{:S(2)}) copy-start(f32[8,16,128]{2,1,0:T(8,128)} %param.15) | copy-start | bytes 196612
  1.6 5.6 %collective-permute-start = (f32[5,2,16,128]{3,2,1,0:T(8,128)S(1)}, f32[5,2,16,128]{3,2,1,0:T(8,128)S(1)}, u32[]{:S(2)}, u32[]{:S(2)}) collective-permute-start(f32[5,2,16,128]{3,2,1,0:T(8,128)S(1)} %get-tuple-element.122), channel_id=1, source_target_pairs={{0,8},{8,16},{16,24},{1,9},{9,17},{17,25},{2,10},{10,18},{18,26},{... | collective-permute-start | bytes 245768 | tf_op jit(solution)/shard_map/ppermute | solution.py:19
  5.3 5.8 %collective-permute-start.1 = (f32[5,2,16,128]{3,2,1,0:T(8,128)S(1)}, f32[5,2,16,128]{3,2,1,0:T(8,128)S(1)}, u32[]{:S(2)}, u32[]{:S(2)}) collective-permute-start(f32[5,2,16,128]{3,2,1,0:T(8,128)S(1)} %get-tuple-element.123), channel_id=1, source_target_pairs={{8,0},{16,8},{24,16},{9,1},{17,9},{25,17},{10,2},{18,10},{26,18},{... | collective-permute-start | bytes 245768 | tf_op jit(solution)/shard_map/ppermute | solution.py:20
  12.1 15.0 %collective-permute-start.2 = (f32[5,12,2,128]{3,2,1,0:T(2,128)S(1)}, f32[5,12,2,128]{3,2,1,0:T(2,128)S(1)}, u32[]{:S(2)}, u32[]{:S(2)}) collective-permute-start(f32[5,12,2,128]{3,2,1,0:T(2,128)S(1)} %get-tuple-element.108), channel_id=1, source_target_pairs={{0,4},{1,5},{2,6},{3,7},{8,12},{9,13},{10,14},{11,15},{16,20},{17,... | collective-permute-start | bytes 184328 | tf_op jit(solution)/shard_map/ppermute | solution.py:19
  15.3 11.9 %collective-permute-start.3 = (f32[5,12,2,128]{3,2,1,0:T(2,128)S(1)}, f32[5,12,2,128]{3,2,1,0:T(2,128)S(1)}, u32[]{:S(2)}, u32[]{:S(2)}) collective-permute-start(f32[5,12,2,128]{3,2,1,0:T(2,128)S(1)} %get-tuple-element.109), channel_id=1, source_target_pairs={{4,0},{5,1},{6,2},{7,3},{12,8},{13,9},{14,10},{15,11},{20,16},{21,... | collective-permute-start | bytes 184328 | tf_op jit(solution)/shard_map/ppermute | solution.py:20
  24.5 2.6 copy-start
  28.0 44.4 %collective-permute-start.4 = (f32[5,12,20,2]{2,3,1,0:T(2,128)S(1)}, f32[5,12,20,2]{2,3,1,0:T(2,128)S(1)}, u32[]{:S(2)}, u32[]{:S(2)}) collective-permute-start(f32[5,12,20,2]{2,3,1,0:T(2,128)S(1)} %copy.766), channel_id=1, source_target_pairs={{0,1},{1,2},{2,3},{4,5},{5,6},{6,7},{8,9},{9,10},{10,11},{12,13},{... | collective-permute-start | bytes 28808 | tf_op jit(solution)/shard_map/ppermute | solution.py:19
  29.8 43.1 %collective-permute-start.5 = (f32[5,12,20,2]{2,3,1,0:T(2,128)S(1)}, f32[5,12,20,2]{2,3,1,0:T(2,128)S(1)}, u32[]{:S(2)}, u32[]{:S(2)}) collective-permute-start(f32[5,12,20,2]{2,3,1,0:T(2,128)S(1)} %copy.767), channel_id=1, source_target_pairs={{1,0},{2,1},{3,2},{5,4},{6,5},{7,6},{9,8},{10,9},{11,10},{13,12},{... | collective-permute-start | bytes 28808 | tf_op jit(solution)/shard_map/ppermute | solution.py:20
  90.4 7.9 %copy-start.5 = (f32[4,8,16,128]{3,2,1,0:T(8,128)S(1)}, f32[4,8,16,128]{3,2,1,0:T(8,128)}, u32[]{:S(2)}) copy-start(f32[4,8,16,128]{3,2,1,0:T(8,128)} %param.13) | copy-start | bytes 786436
  90.4 7.9 %copy-start.6 = (f32[4,8,16,128]{3,2,1,0:T(8,128)S(1)}, f32[4,8,16,128]{3,2,1,0:T(8,128)}, u32[]{:S(2)}) copy-start(f32[4,8,16,128]{3,2,1,0:T(8,128)} %param.12) | copy-start | bytes 786436
  90.8 8.9 %collective-permute-start.6 = (f32[5,2,8,64]{3,2,1,0:T(8,128)S(1)}, f32[5,2,8,64]{3,2,1,0:T(8,128)S(1)}, u32[]{:S(2)}, u32[]{:S(2)}) collective-permute-start(f32[5,2,8,64]{3,2,1,0:T(8,128)S(1)} %get-tuple-element.154), channel_id=1, source_target_pairs={{0,8},{8,16},{16,24},{1,9},{9,17},{17,25},{2,10},{10,18},{18,26},{... | collective-permute-start | bytes 61448 | tf_op jit(solution)/shard_map/ppermute | solution.py:19
  96.1 5.3 %collective-permute-start.7 = (f32[5,2,8,64]{3,2,1,0:T(8,128)S(1)}, f32[5,2,8,64]{3,2,1,0:T(8,128)S(1)}, u32[]{:S(2)}, u32[]{:S(2)}) collective-permute-start(f32[5,2,8,64]{3,2,1,0:T(8,128)S(1)} %get-tuple-element.155), channel_id=1, source_target_pairs={{8,0},{16,8},{24,16},{9,1},{17,9},{25,17},{10,2},{18,10},{26,18},{... | collective-permute-start | bytes 61448 | tf_op jit(solution)/shard_map/ppermute | solution.py:20
  99.0 14.4 %copy-start.2 = (f32[4,8,16,128]{3,0,2,1:T(4,128)}, f32[4,8,16,128]{3,0,2,1:T(4,128)S(1)}, u32[]{:S(2)}) copy-start(f32[4,8,16,128]{3,0,2,1:T(4,128)S(1)} %convolution_subtract_fusion) | copy-start | bytes 786436
  101.5 3.1 collective-permute-start.8
  103.2 4.7 %collective-permute-start.9 = (f32[5,8,2,64]{3,1,2,0:T(8,128)S(1)}, f32[5,8,2,64]{3,1,2,0:T(8,128)S(1)}, u32[]{:S(2)}, u32[]{:S(2)}) collective-permute-start(f32[5,8,2,64]{3,1,2,0:T(8,128)S(1)} %copy.839), channel_id=1, source_target_pairs={{4,0},{5,1},{6,2},{7,3},{12,8},{13,9},{14,10},{15,11},{20,16},{21,... | collective-permute-start | bytes 61448 | tf_op jit(solution)/shard_map/ppermute | solution.py:20
  108.1 9.3 %collective-permute-start.10 = (f32[5,8,12,2]{3,1,2,0:T(8,128)S(1)}, f32[5,8,12,2]{3,1,2,0:T(8,128)S(1)}, u32[]{:S(2)}, u32[]{:S(2)}) collective-permute-start(f32[5,8,12,2]{3,1,2,0:T(8,128)S(1)} %get-tuple-element.130), channel_id=1, source_target_pairs={{0,1},{1,2},{2,3},{4,5},{5,6},{6,7},{8,9},{9,10},{10,11},{12,13},{... | collective-permute-start | bytes 11528 | tf_op jit(solution)/shard_map/ppermute | solution.py:19
  109.4 9.7 %collective-permute-start.11 = (f32[5,8,12,2]{3,1,2,0:T(8,128)S(1)}, f32[5,8,12,2]{3,1,2,0:T(8,128)S(1)}, u32[]{:S(2)}, u32[]{:S(2)}) collective-permute-start(f32[5,8,12,2]{3,1,2,0:T(8,128)S(1)} %get-tuple-element.131), channel_id=1, source_target_pairs={{1,0},{2,1},{3,2},{5,4},{6,5},{7,6},{9,8},{10,9},{11,10},{13,12},{... | collective-permute-start | bytes 11528 | tf_op jit(solution)/shard_map/ppermute | solution.py:20
  121.7 42.9 %collective-permute-start.12 = (f32[5,2,4,32]{3,2,1,0:T(4,128)S(1)}, f32[5,2,4,32]{3,2,1,0:T(4,128)S(1)}, u32[]{:S(2)}, u32[]{:S(2)}) collective-permute-start(f32[5,2,4,32]{3,2,1,0:T(4,128)S(1)} %pad_maximum_fusion.50), channel_id=1, source_target_pairs={{0,8},{8,16},{16,24},{1,9},{9,17},{17,25},{2,10},{10,18},{18,26},{... | collective-permute-start | bytes 15368 | tf_op jit(solution)/shard_map/ppermute | solution.py:19
  123.6 41.0 %collective-permute-start.13 = (f32[5,2,4,32]{3,2,1,0:T(4,128)S(1)}, f32[5,2,4,32]{3,2,1,0:T(4,128)S(1)}, u32[]{:S(2)}, u32[]{:S(2)}) collective-permute-start(f32[5,2,4,32]{3,2,1,0:T(4,128)S(1)} %pad_maximum_fusion.50), channel_id=1, source_target_pairs={{8,0},{16,8},{24,16},{9,1},{17,9},{25,17},{10,2},{18,10},{26,18},{... | collective-permute-start | bytes 15368 | tf_op jit(solution)/shard_map/ppermute | solution.py:20
  164.7 5.8 %collective-permute-start.14 = (f32[5,6,2,32]{3,2,1,0:T(2,128)S(1)}, f32[5,6,2,32]{3,2,1,0:T(2,128)S(1)}, u32[]{:S(2)}, u32[]{:S(2)}) collective-permute-start(f32[5,6,2,32]{3,2,1,0:T(2,128)S(1)} %get-tuple-element.158), channel_id=1, source_target_pairs={{0,4},{1,5},{2,6},{3,7},{8,12},{9,13},{10,14},{11,15},{16,20},{17,... | collective-permute-start | bytes 23048 | tf_op jit(solution)/shard_map/ppermute | solution.py:19
  169.0 4.6 %collective-permute-start.15 = (f32[5,6,2,32]{3,2,1,0:T(2,128)S(1)}, f32[5,6,2,32]{3,2,1,0:T(2,128)S(1)}, u32[]{:S(2)}, u32[]{:S(2)}) collective-permute-start(f32[5,6,2,32]{3,2,1,0:T(2,128)S(1)} %get-tuple-element.159), channel_id=1, source_target_pairs={{4,0},{5,1},{6,2},{7,3},{12,8},{13,9},{14,10},{15,11},{20,16},{21,... | collective-permute-start | bytes 23048 | tf_op jit(solution)/shard_map/ppermute | solution.py:20
  173.8 5.6 %collective-permute-start.16 = (f32[5,6,8,2]{3,2,1,0:T(8,128)S(1)}, f32[5,6,8,2]{3,2,1,0:T(8,128)S(1)}, u32[]{:S(2)}, u32[]{:S(2)}) collective-permute-start(f32[5,6,8,2]{3,2,1,0:T(8,128)S(1)} %get-tuple-element.150), channel_id=1, source_target_pairs={{0,1},{1,2},{2,3},{4,5},{5,6},{6,7},{8,9},{9,10},{10,11},{12,13},{... | collective-permute-start | bytes 5768 | tf_op jit(solution)/shard_map/ppermute | solution.py:19
  175.1 5.8 %collective-permute-start.17 = (f32[5,6,8,2]{3,2,1,0:T(8,128)S(1)}, f32[5,6,8,2]{3,2,1,0:T(8,128)S(1)}, u32[]{:S(2)}, u32[]{:S(2)}) collective-permute-start(f32[5,6,8,2]{3,2,1,0:T(8,128)S(1)} %get-tuple-element.151), channel_id=1, source_target_pairs={{1,0},{2,1},{3,2},{5,4},{6,5},{7,6},{9,8},{10,9},{11,10},{13,12},{... | collective-permute-start | bytes 5768 | tf_op jit(solution)/shard_map/ppermute | solution.py:20
  247.3 12.6 %collective-permute-start.18 = (f32[4,1,4,32]{3,2,1,0:T(4,128)S(1)}, f32[4,1,4,32]{3,2,1,0:T(4,128)S(1)}, u32[]{:S(2)}, u32[]{:S(2)}) collective-permute-start(f32[4,1,4,32]{3,2,1,0:T(4,128)S(1)} %get-tuple-element.175), channel_id=1, source_target_pairs={{8,0},{16,8},{24,16},{9,1},{17,9},{25,17},{10,2},{18,10},{26,18},{... | collective-permute-start | bytes 6152 | tf_op jit(solution)/shard_map/ppermute | solution.py:20
  256.0 4.3 %collective-permute-start.19 = (f32[4,1,4,32]{3,2,1,0:T(4,128)S(1)}, f32[4,1,4,32]{3,2,1,0:T(4,128)S(1)}, u32[]{:S(2)}, u32[]{:S(2)}) collective-permute-start(f32[4,1,4,32]{3,2,1,0:T(4,128)S(1)} %get-tuple-element.174), channel_id=1, source_target_pairs={{0,8},{8,16},{16,24},{1,9},{9,17},{17,25},{2,10},{10,18},{18,26},{... | collective-permute-start | bytes 6152 | tf_op jit(solution)/shard_map/ppermute | solution.py:19
  260.3 4.6 %collective-permute-start.21 = (f32[4,4,1,32]{3,2,1,0:T(1,128)S(1)}, f32[4,4,1,32]{3,2,1,0:T(1,128)S(1)}, u32[]{:S(2)}, u32[]{:S(2)}) collective-permute-start(f32[4,4,1,32]{3,2,1,0:T(1,128)S(1)} %get-tuple-element.167), channel_id=1, source_target_pairs={{0,4},{1,5},{2,6},{3,7},{8,12},{9,13},{10,14},{11,15},{16,20},{17,... | collective-permute-start | bytes 6152 | tf_op jit(solution)/shard_map/ppermute | solution.py:19
  263.6 4.4 %collective-permute-start.20 = (f32[4,4,1,32]{3,2,1,0:T(1,128)S(1)}, f32[4,4,1,32]{3,2,1,0:T(1,128)S(1)}, u32[]{:S(2)}, u32[]{:S(2)}) collective-permute-start(f32[4,4,1,32]{3,2,1,0:T(1,128)S(1)} %get-tuple-element.166), channel_id=1, source_target_pairs={{4,0},{5,1},{6,2},{7,3},{12,8},{13,9},{14,10},{15,11},{20,16},{21,... | collective-permute-start | bytes 6152 | tf_op jit(solution)/shard_map/ppermute | solution.py:20
  268.1 3.6 collective-permute-start.22
  269.7 6.2 %collective-permute-start.23 = (f32[4,4,6,1]{3,1,2,0:T(4,128)S(1)}, f32[4,4,6,1]{3,1,2,0:T(4,128)S(1)}, u32[]{:S(2)}, u32[]{:S(2)}) collective-permute-start(f32[4,4,6,1]{3,1,2,0:T(4,128)S(1)} %get-tuple-element.163), channel_id=1, source_target_pairs={{0,1},{1,2},{2,3},{4,5},{5,6},{6,7},{8,9},{9,10},{10,11},{12,13},{... | collective-permute-start | bytes 1160 | tf_op jit(solution)/shard_map/ppermute | solution.py:19
  276.8 8.8 %collective-permute-start.24 = (f32[4,1,8,64]{3,2,1,0:T(8,128)S(1)}, f32[4,1,8,64]{3,2,1,0:T(8,128)S(1)}, u32[]{:S(2)}, u32[]{:S(2)}) collective-permute-start(f32[4,1,8,64]{3,2,1,0:T(8,128)S(1)} %get-tuple-element.157), channel_id=1, source_target_pairs={{8,0},{16,8},{24,16},{9,1},{17,9},{25,17},{10,2},{18,10},{26,18},{... | collective-permute-start | bytes 24584 | tf_op jit(solution)/shard_map/ppermute | solution.py:20
  279.6 6.1 %collective-permute-start.25 = (f32[4,1,8,64]{3,2,1,0:T(8,128)S(1)}, f32[4,1,8,64]{3,2,1,0:T(8,128)S(1)}, u32[]{:S(2)}, u32[]{:S(2)}) collective-permute-start(f32[4,1,8,64]{3,2,1,0:T(8,128)S(1)} %get-tuple-element.156), channel_id=1, source_target_pairs={{0,8},{8,16},{16,24},{1,9},{9,17},{17,25},{2,10},{10,18},{18,26},{... | collective-permute-start | bytes 24584 | tf_op jit(solution)/shard_map/ppermute | solution.py:19
  285.8 3.3 collective-permute-start.27
  287.8 4.4 %collective-permute-start.26 = (f32[4,6,1,64]{3,0,2,1:T(4,128)S(1)}, f32[4,6,1,64]{3,0,2,1:T(4,128)S(1)}, u32[]{:S(2)}, u32[]{:S(2)}) collective-permute-start(f32[4,6,1,64]{3,0,2,1:T(4,128)S(1)} %copy.732), channel_id=1, source_target_pairs={{4,0},{5,1},{6,2},{7,3},{12,8},{13,9},{14,10},{15,11},{20,16},{21,... | collective-permute-start | bytes 18440 | tf_op jit(solution)/shard_map/ppermute | solution.py:20
  292.4 5.8 %collective-permute-start.28 = (f32[4,6,10,1]{3,0,2,1:T(4,128)S(1)}, f32[4,6,10,1]{3,0,2,1:T(4,128)S(1)}, u32[]{:S(2)}, u32[]{:S(2)}) collective-permute-start(f32[4,6,10,1]{3,0,2,1:T(4,128)S(1)} %get-tuple-element.146), channel_id=1, source_target_pairs={{1,0},{2,1},{3,2},{5,4},{6,5},{7,6},{9,8},{10,9},{11,10},{13,12},{... | collective-permute-start | bytes 2888 | tf_op jit(solution)/shard_map/ppermute | solution.py:20
  296.1 6.2 %collective-permute-start.29 = (f32[4,6,10,1]{3,0,2,1:T(4,128)S(1)}, f32[4,6,10,1]{3,0,2,1:T(4,128)S(1)}, u32[]{:S(2)}, u32[]{:S(2)}) collective-permute-start(f32[4,6,10,1]{3,0,2,1:T(4,128)S(1)} %get-tuple-element.147), channel_id=1, source_target_pairs={{0,1},{1,2},{2,3},{4,5},{5,6},{6,7},{8,9},{9,10},{10,11},{12,13},{... | collective-permute-start | bytes 2888 | tf_op jit(solution)/shard_map/ppermute | solution.py:19
  307.8 10.6 %collective-permute-start.30 = (f32[4,1,16,128]{3,2,1,0:T(8,128)S(1)}, f32[4,1,16,128]{3,2,1,0:T(8,128)S(1)}, u32[]{:S(2)}, u32[]{:S(2)}) collective-permute-start(f32[4,1,16,128]{3,2,1,0:T(8,128)S(1)} %get-tuple-element.129), channel_id=1, source_target_pairs={{8,0},{16,8},{24,16},{9,1},{17,9},{25,17},{10,2},{18,10},{26,18},{... | collective-permute-start | bytes 98312 | tf_op jit(solution)/shard_map/ppermute | solution.py:20
  309.8 8.7 %collective-permute-start.31 = (f32[4,1,16,128]{3,2,1,0:T(8,128)S(1)}, f32[4,1,16,128]{3,2,1,0:T(8,128)S(1)}, u32[]{:S(2)}, u32[]{:S(2)}) collective-permute-start(f32[4,1,16,128]{3,2,1,0:T(8,128)S(1)} %get-tuple-element.128), channel_id=1, source_target_pairs={{0,8},{8,16},{16,24},{1,9},{9,17},{17,25},{2,10},{10,18},{18,26},{... | collective-permute-start | bytes 98312 | tf_op jit(solution)/shard_map/ppermute | solution.py:19
  318.5 3.5 collective-permute-start.33
  320.7 4.5 %collective-permute-start.32 = (f32[4,10,1,128]{3,0,2,1:T(4,128)S(1)}, f32[4,10,1,128]{3,0,2,1:T(4,128)S(1)}, u32[]{:S(2)}, u32[]{:S(2)}) collective-permute-start(f32[4,10,1,128]{3,0,2,1:T(4,128)S(1)} %copy.742), channel_id=1, source_target_pairs={{4,0},{5,1},{6,2},{7,3},{12,8},{13,9},{14,10},{15,11},{20,16},{21,... | collective-permute-start | bytes 61448 | tf_op jit(solution)/shard_map/ppermute | solution.py:20
  325.5 9.9 %collective-permute-start.34 = (f32[4,10,18,1]{3,0,2,1:T(4,128)S(1)}, f32[4,10,18,1]{3,0,2,1:T(4,128)S(1)}, u32[]{:S(2)}, u32[]{:S(2)}) collective-permute-start(f32[4,10,18,1]{3,0,2,1:T(4,128)S(1)} %get-tuple-element.116), channel_id=1, source_target_pairs={{1,0},{2,1},{3,2},{5,4},{6,5},{7,6},{9,8},{10,9},{11,10},{13,12},{... | collective-permute-start | bytes 8648 | tf_op jit(solution)/shard_map/ppermute | solution.py:20
  329.2 10.3 %collective-permute-start.35 = (f32[4,10,18,1]{3,0,2,1:T(4,128)S(1)}, f32[4,10,18,1]{3,0,2,1:T(4,128)S(1)}, u32[]{:S(2)}, u32[]{:S(2)}) collective-permute-start(f32[4,10,18,1]{3,0,2,1:T(4,128)S(1)} %get-tuple-element.117), channel_id=1, source_target_pairs={{0,1},{1,2},{2,3},{4,5},{5,6},{6,7},{8,9},{9,10},{10,11},{12,13},{... | collective-permute-start | bytes 8648 | tf_op jit(solution)/shard_map/ppermute | solution.py:19
  331.3 14.8 %copy-start.3 = (f32[4,8,16,128]{3,0,2,1:T(4,128)S(1)}, f32[4,8,16,128]{3,0,2,1:T(4,128)}, u32[]{:S(2)}) copy-start(f32[4,8,16,128]{3,0,2,1:T(4,128)} %copy-done.2) | copy-start | bytes 786436
  340.2 28.9 %copy-start.4 = (f32[4,8,16,128]{3,2,1,0:T(8,128)}, f32[4,8,16,128]{3,2,1,0:T(8,128)S(1)}, u32[]{:S(2)}) copy-start(f32[4,8,16,128]{3,2,1,0:T(8,128)S(1)} %fusion.30) | copy-start | bytes 786436
  340.2 6.6 %collective-permute-start.36 = (f32[4,1,16,128]{3,2,1,0:T(8,128)S(1)}, f32[4,1,16,128]{3,2,1,0:T(8,128)S(1)}, u32[]{:S(2)}, u32[]{:S(2)}) collective-permute-start(f32[4,1,16,128]{3,2,1,0:T(8,128)S(1)} %get-tuple-element.127), channel_id=1, source_target_pairs={{8,0},{16,8},{24,16},{9,1},{17,9},{25,17},{10,2},{18,10},{26,18},{... | collective-permute-start | bytes 98312 | tf_op jit(solution)/shard_map/ppermute | solution.py:20
  342.1 5.1 %collective-permute-start.37 = (f32[4,1,16,128]{3,2,1,0:T(8,128)S(1)}, f32[4,1,16,128]{3,2,1,0:T(8,128)S(1)}, u32[]{:S(2)}, u32[]{:S(2)}) collective-permute-start(f32[4,1,16,128]{3,2,1,0:T(8,128)S(1)} %get-tuple-element.126), channel_id=1, source_target_pairs={{0,8},{8,16},{16,24},{1,9},{9,17},{17,25},{2,10},{10,18},{18,26},{... | collective-permute-start | bytes 98312 | tf_op jit(solution)/shard_map/ppermute | solution.py:19
  347.3 3.4 collective-permute-start.39
  349.4 4.5 %collective-permute-start.38 = (f32[4,10,1,128]{3,0,2,1:T(4,128)S(1)}, f32[4,10,1,128]{3,0,2,1:T(4,128)S(1)}, u32[]{:S(2)}, u32[]{:S(2)}) collective-permute-start(f32[4,10,1,128]{3,0,2,1:T(4,128)S(1)} %copy.749), channel_id=1, source_target_pairs={{4,0},{5,1},{6,2},{7,3},{12,8},{13,9},{14,10},{15,11},{20,16},{21,... | collective-permute-start | bytes 61448 | tf_op jit(solution)/shard_map/ppermute | solution.py:20
  354.2 10.0 %collective-permute-start.40 = (f32[4,10,18,1]{3,0,2,1:T(4,128)S(1)}, f32[4,10,18,1]{3,0,2,1:T(4,128)S(1)}, u32[]{:S(2)}, u32[]{:S(2)}) collective-permute-start(f32[4,10,18,1]{3,0,2,1:T(4,128)S(1)} %get-tuple-element.112), channel_id=1, source_target_pairs={{1,0},{2,1},{3,2},{5,4},{6,5},{7,6},{9,8},{10,9},{11,10},{13,12},{... | collective-permute-start | bytes 8648 | tf_op jit(solution)/shard_map/ppermute | solution.py:20
  356.1 12.5 %collective-permute-start.41 = (f32[4,10,18,1]{3,0,2,1:T(4,128)S(1)}, f32[4,10,18,1]{3,0,2,1:T(4,128)S(1)}, u32[]{:S(2)}, u32[]{:S(2)}) collective-permute-start(f32[4,10,18,1]{3,0,2,1:T(4,128)S(1)} %get-tuple-element.113), channel_id=1, source_target_pairs={{0,1},{1,2},{2,3},{4,5},{5,6},{6,7},{8,9},{9,10},{10,11},{12,13},{... | collective-permute-start | bytes 8648 | tf_op jit(solution)/shard_map/ppermute | solution.py:19
where the time goes:
time: 371 us; the launch traced here: 370 us
  blocking collectives  138 us (37%)
  starting transfers between devices  110 us (30%)
  waiting for transfers between devices  57.7 us (16%)
  other arithmetic  29.1 us (8%)
  local copies, waits for them, and re-layouts  26.4 us (7%)
  matrix products  6.55 us (2%)
    all_gather x1, blocking collectives, agglomerate(): gathered = lax.all_gather(flattened, ('gx', 'gy', 'gz'), axis=1, tiled=True)  61.1 us
    ppermute x21, starting transfers between devices, with_halo(): before = lax.ppermute(last, axis, up)  56.1 us
    ppermute x21, starting transfers between devices, with_halo(): after = lax.ppermute(leading, axis, down)  53.7 us
    psum x1, blocking collectives, per_device(): projection = lax.psum(basis_local, ('gx', 'gy', 'gz')) / total_cells  38.6 us
    psum x1, blocking collectives, per_device(): gram = lax.psum(gram_local, ('gx', 'gy', 'gz')) / total_cells  38.6 us
    ppermute x21, waiting for transfers between devices, with_halo(): after = lax.ppermute(leading, axis, down)  36.8 us
    ppermute x21, waiting for transfers between devices, with_halo(): before = lax.ppermute(last, axis, up)  20.8 us
    reduce_sum x14, other arithmetic, restrict(): field.reshape(depth, size_a // 2, 2, size_b // 2, 2, size_c // 2, 2)  13 us
  transfers between devices with their start and end apart: 42, of which 22 were waited for; matrix products, arithmetic and copies ran while one was open for 7% of the time, Pallas kernels for 0%

commit v1 on v0

--- a/solution.py
+++ b/solution.py
@@ -71,7 +71,8 @@
     stacked = jnp.concatenate([source, coeffs[None]], axis=0)
     depth, size_a, size_b, size_c = stacked.shape
     flattened = stacked.reshape(depth, size_a * size_b * size_c)
-    gathered = lax.all_gather(flattened, ("gx", "gy", "gz"), axis=1, tiled=True)
+    shards = lax.all_gather(flattened, ("gx", "gy", "gz"))
+    gathered = jnp.concatenate(shards, axis=1)
     count_x, count_y, count_z = (lax.axis_size("gx"), lax.axis_size("gy"), lax.axis_size("gz"))
     gathered = gathered.reshape(depth, count_x, count_y, count_z, size_a, size_b, size_c)
     gathered = gathered.transpose(0, 1, 4, 2, 5, 3, 6).reshape(

time: 371 us -> 371 us (level)
  no operation moved by 1% of the time
where the time goes in v1:
time: 371 us; the launch traced here: 370 us
  blocking collectives  138 us (37%)
  starting transfers between devices  110 us (30%)
  waiting for transfers between devices  57.7 us (16%)
  other arithmetic  29.1 us (8%)
  local copies, waits for them, and re-layouts  26.4 us (7%)
  matrix products  6.54 us (2%)
    all_gather x1, blocking collectives, agglomerate(): shards = lax.all_gather(flattened, ('gx', 'gy', 'gz'))  61.1 us
    ppermute x21, starting transfers between devices, with_halo(): before = lax.ppermute(last, axis, up)  55.9 us
    ppermute x21, starting transfers between devices, with_halo(): after = lax.ppermute(leading, axis, down)  53.7 us
    psum x1, blocking collectives, per_device(): projection = lax.psum(basis_local, ('gx', 'gy', 'gz')) / total_cells  38.6 us
    psum x1, blocking collectives, per_device(): gram = lax.psum(gram_local, ('gx', 'gy', 'gz')) / total_cells  38.6 us
    ppermute x21, waiting for transfers between devices, with_halo(): after = lax.ppermute(leading, axis, down)  36.8 us
    ppermute x21, waiting for transfers between devices, with_halo(): before = lax.ppermute(last, axis, up)  20.8 us
    reduce_sum x14, other arithmetic, restrict(): field.reshape(depth, size_a // 2, 2, size_b // 2, 2, size_c // 2, 2)  13 us
  transfers between devices with their start and end apart: 42, of which 22 were waited for; matrix products, arithmetic and copies ran while one was open for 7% of the time, Pallas kernels for 0%

profile of v1, /device:TPU:25, one launch (start us, length us, event | category | flops | bytes accessed | tf_op | source)
XLA Modules:
  0.0 369.7 jit_solution(18117572034051456794)
XLA Ops:
  1.6 3.7 %collective-permute-start = (f32[5,2,16,128]{3,2,1,0:T(8,128)S(1)}, f32[5,2,16,128]{3,2,1,0:T(8,128)S(1)}, u32[]{:S(2)}, u32[]{:S(2)}) collective-permute-start(f32[5,2,16,128]{3,2,1,0:T(8,128)S(1)} %get-tuple-element.122), channel_id=1, source_target_pairs={{0,8},{8,16},{16,24},{1,9},{9,17},{17,25},{2,10},{10,18},{18,26},{... | collective-permute-start | bytes 245768 | tf_op jit(solution)/shard_map/ppermute | solution.py:19
  5.3 1.9 collective-permute-start.1
  7.3 3.8 %collective-permute-done.1 = f32[5,2,16,128]{3,2,1,0:T(8,128)S(1)} collective-permute-done((f32[5,2,16,128]{3,2,1,0:T(8,128)S(1)}, f32[5,2,16,128]{3,2,1,0:T(8,128)S(1)}, u32[]{:S(2)}, u32[]{:S(2)}) %collective-permute-start.1) | collective-permute-done | bytes 81952 | tf_op jit(solution)/shard_map/ppermute | solution.py:20
  12.1 3.1 collective-permute-start.2
  15.3 1.3 collective-permute-start.3
  16.6 2.4 convolution_bitcast_fusion.1
  19.0 5.5 %reshape_broadcast_in_dim.3 = f32[4,2,8,2,64,2]{5,4,3,2,1,0:T(8,128)} reshape(f32[8,16,128]{2,1,0:T(8,128)S(1)} %copy-done.1) | data formatting | bytes 131072 | tf_op jit(solution)/shard_map/reshape;broadcast_in_dim | solution.py:43
  24.5 2.6 reduce_sum.103
  29.8 4.0 %collective-permute-start.5 = (f32[5,12,20,2]{2,3,1,0:T(2,128)S(1)}, f32[5,12,20,2]{2,3,1,0:T(2,128)S(1)}, u32[]{:S(2)}, u32[]{:S(2)}) collective-permute-start(f32[5,12,20,2]{2,3,1,0:T(2,128)S(1)} %copy.774), channel_id=1, source_target_pairs={{1,0},{2,1},{3,2},{5,4},{6,5},{7,6},{9,8},{10,9},{11,10},{13,12},{... | collective-permute-start | bytes 28808 | tf_op jit(solution)/shard_map/ppermute | solution.py:20
  33.8 38.6 %psum.14 = f32[4,4]{0,1:T(4,128)S(1)} all-reduce(f32[4,4]{0,1:T(4,128)S(1)} %convolution_bitcast_fusion.1), channel_id=1, replica_groups=mesh['gx'=4,'gy'=2,'gz'=4] {'gx','gy','gz'}, use_global_device_ids=true, to_apply=%region_0.0 | all-reduce | flops 16 | bytes 128 | tf_op jit(solution)/shard_map/psum | solution.py:135
  74.6 1.9 fusion.12
  77.0 4.7 %copy.695 = f32[4,8,16,128]{0,3,2,1:T(8,128)} copy(f32[4,8,16,128]{3,2,1,0:T(8,128)S(1)} %fusion.35) | data formatting | bytes 524288 | tf_op jit(solution)/shard_map/sub | solution.py:113
  81.7 8.7 %reduce_sum.102 = f32[4,4,8,64]{0,3,2,1:T(8,128)S(1)} reduce(f32[4,4,2,8,2,64,2]{0,6,5,4,3,2,1:T(2,128)} %bitcast.126, f32[]{:T(128)} %constant.248.clone.1), dimensions={2,4,6}, to_apply=%region_4.0 | reduce | flops 57344 | bytes 294916 | tf_op jit(solution)/shard_map/reduce_sum | solution.py:43
  90.8 5.3 %collective-permute-start.6 = (f32[5,2,8,64]{3,2,1,0:T(8,128)S(1)}, f32[5,2,8,64]{3,2,1,0:T(8,128)S(1)}, u32[]{:S(2)}, u32[]{:S(2)}) collective-permute-start(f32[5,2,8,64]{3,2,1,0:T(8,128)S(1)} %get-tuple-element.154), channel_id=1, source_target_pairs={{0,8},{8,16},{16,24},{1,9},{9,17},{17,25},{2,10},{10,18},{18,26},{... | collective-permute-start | bytes 61448 | tf_op jit(solution)/shard_map/ppermute | solution.py:19
  96.1 2.1 collective-permute-start.7
  99.7 1.7 collective-permute-done.7
  101.5 1.8 collective-permute-start.8
  103.2 1.3 collective-permute-start.9
  104.6 3.4 collective-permute-done.9
  108.1 1.3 collective-permute-start.10
  109.4 4.0 %collective-permute-start.11 = (f32[5,8,12,2]{3,1,2,0:T(8,128)S(1)}, f32[5,8,12,2]{3,1,2,0:T(8,128)S(1)}, u32[]{:S(2)}, u32[]{:S(2)}) collective-permute-start(f32[5,8,12,2]{3,1,2,0:T(8,128)S(1)} %get-tuple-element.131), channel_id=1, source_target_pairs={{1,0},{2,1},{3,2},{5,4},{6,5},{7,6},{9,8},{10,9},{11,10},{13,12},{... | collective-permute-start | bytes 11528 | tf_op jit(solution)/shard_map/ppermute | solution.py:20
  114.7 2.7 collective-permute-done.10
  117.4 1.8 collective-permute-done.11
  121.7 1.9 collective-permute-start.12
  123.6 2.4 collective-permute-start.13
  126.0 38.6 %psum.15 = f32[4,4]{0,1:T(4,128)S(1)} all-reduce(f32[4,4]{0,1:T(4,128)S(1)} %convolution_bitcast_fusion), channel_id=1, replica_groups=mesh['gx'=4,'gy'=2,'gz'=4] {'gx','gy','gz'}, use_global_device_ids=true, to_apply=%region_1.0 | all-reduce | flops 16 | bytes 128 | tf_op jit(solution)/shard_map/psum | solution.py:138
  164.7 4.3 %collective-permute-start.14 = (f32[5,6,2,32]{3,2,1,0:T(2,128)S(1)}, f32[5,6,2,32]{3,2,1,0:T(2,128)S(1)}, u32[]{:S(2)}, u32[]{:S(2)}) collective-permute-start(f32[5,6,2,32]{3,2,1,0:T(2,128)S(1)} %get-tuple-element.158), channel_id=1, source_target_pairs={{0,4},{1,5},{2,6},{3,7},{8,12},{9,13},{10,14},{11,15},{16,20},{17,... | collective-permute-start | bytes 23048 | tf_op jit(solution)/shard_map/ppermute | solution.py:19
  169.0 1.3 collective-permute-start.15
  170.5 3.1 collective-permute-done.15
  173.8 1.3 collective-permute-start.16
  175.1 4.0 %collective-permute-start.17 = (f32[5,6,8,2]{3,2,1,0:T(8,128)S(1)}, f32[5,6,8,2]{3,2,1,0:T(8,128)S(1)}, u32[]{:S(2)}, u32[]{:S(2)}) collective-permute-start(f32[5,6,8,2]{3,2,1,0:T(8,128)S(1)} %get-tuple-element.151), channel_id=1, source_target_pairs={{1,0},{2,1},{3,2},{5,4},{6,5},{7,6},{9,8},{10,9},{11,10},{13,12},{... | collective-permute-start | bytes 5768 | tf_op jit(solution)/shard_map/ppermute | solution.py:20
  179.4 1.5 collective-permute-done.17
  181.9 61.1 %all_gather.3 = f32[32,5,32]{2,1,0:T(8,128)S(1)} all-gather(f32[1,5,32]{2,1,0:T(8,128)S(1)} %pad_maximum_fusion.65), channel_id=1, replica_groups=mesh['gx'=4,'gy'=2,'gz'=4] {'gx','gy','gz'}, dimensions={0}, use_global_device_ids=true | all-gather | bytes 21120 | tf_op jit(solution)/shard_map/all_gather | solution.py:74
  247.1 8.6 %collective-permute-start.18 = (f32[4,1,4,32]{3,2,1,0:T(4,128)S(1)}, f32[4,1,4,32]{3,2,1,0:T(4,128)S(1)}, u32[]{:S(2)}, u32[]{:S(2)}) collective-permute-start(f32[4,1,4,32]{3,2,1,0:T(4,128)S(1)} %get-tuple-element.175), channel_id=1, source_target_pairs={{8,0},{16,8},{24,16},{9,1},{17,9},{25,17},{10,2},{18,10},{26,18},{... | collective-permute-start | bytes 6152 | tf_op jit(solution)/shard_map/ppermute | solution.py:20
  255.7 3.6 collective-permute-start.19
  260.1 3.2 collective-permute-start.21
  264.7 3.0 collective-permute-done.20
  267.8 1.7 collective-permute-start.22
  271.5 4.3 %collective-permute-done.23 = f32[4,4,6,1]{3,1,2,0:T(4,128)S(1)} collective-permute-done((f32[4,4,6,1]{3,1,2,0:T(4,128)S(1)}, f32[4,4,6,1]{3,1,2,0:T(4,128)S(1)}, u32[]{:S(2)}, u32[]{:S(2)}) %collective-permute-start.23) | collective-permute-done | bytes 416 | tf_op jit(solution)/shard_map/ppermute | solution.py:19
  276.6 2.8 collective-permute-start.24
  279.4 5.3 %collective-permute-start.25 = (f32[4,1,8,64]{3,2,1,0:T(8,128)S(1)}, f32[4,1,8,64]{3,2,1,0:T(8,128)S(1)}, u32[]{:S(2)}, u32[]{:S(2)}) collective-permute-start(f32[4,1,8,64]{3,2,1,0:T(8,128)S(1)} %get-tuple-element.156), channel_id=1, source_target_pairs={{0,8},{8,16},{16,24},{1,9},{9,17},{17,25},{2,10},{10,18},{18,26},{... | collective-permute-start | bytes 24584 | tf_op jit(solution)/shard_map/ppermute | solution.py:19
  285.6 1.4 collective-permute-start.27
  289.0 3.1 collective-permute-done.26
  292.2 3.7 %collective-permute-start.28 = (f32[4,6,10,1]{3,0,2,1:T(4,128)S(1)}, f32[4,6,10,1]{3,0,2,1:T(4,128)S(1)}, u32[]{:S(2)}, u32[]{:S(2)}) collective-permute-start(f32[4,6,10,1]{3,0,2,1:T(4,128)S(1)} %get-tuple-element.146), channel_id=1, source_target_pairs={{1,0},{2,1},{3,2},{5,4},{6,5},{7,6},{9,8},{10,9},{11,10},{13,12},{... | collective-permute-start | bytes 2888 | tf_op jit(solution)/shard_map/ppermute | solution.py:20
  295.9 1.3 collective-permute-start.29
  298.0 4.1 %collective-permute-done.29 = f32[4,6,10,1]{3,0,2,1:T(4,128)S(1)} collective-permute-done((f32[4,6,10,1]{3,0,2,1:T(4,128)S(1)}, f32[4,6,10,1]{3,0,2,1:T(4,128)S(1)}, u32[]{:S(2)}, u32[]{:S(2)}) %collective-permute-start.29) | collective-permute-done | bytes 992 | tf_op jit(solution)/shard_map/ppermute | solution.py:19
  302.5 1.4 copy.745
  303.8 1.4 broadcast_in_dim.131
  305.2 1.3 copy.746
  307.6 1.9 collective-permute-start.30
  309.5 6.5 %collective-permute-start.31 = (f32[4,1,16,128]{3,2,1,0:T(8,128)S(1)}, f32[4,1,16,128]{3,2,1,0:T(8,128)S(1)}, u32[]{:S(2)}, u32[]{:S(2)}) collective-permute-start(f32[4,1,16,128]{3,2,1,0:T(8,128)S(1)} %get-tuple-element.128), channel_id=1, source_target_pairs={{0,8},{8,16},{16,24},{1,9},{9,17},{17,25},{2,10},{10,18},{18,26},{... | collective-permute-start | bytes 98312 | tf_op jit(solution)/shard_map/ppermute | solution.py:19
  316.0 1.9 subtract_divide_fusion
  318.3 1.4 collective-permute-start.33
  322.0 3.0 collective-permute-done.32
  325.3 3.7 collective-permute-start.34
  331.1 4.0 %collective-permute-done.34 = f32[4,10,18,1]{3,0,2,1:T(4,128)S(1)} collective-permute-done((f32[4,10,18,1]{3,0,2,1:T(4,128)S(1)}, f32[4,10,18,1]{3,0,2,1:T(4,128)S(1)}, u32[]{:S(2)}, u32[]{:S(2)}) %collective-permute-start.34) | collective-permute-done | bytes 2912 | tf_op jit(solution)/shard_map/ppermute | solution.py:20
  335.2 4.1 %collective-permute-done.35 = f32[4,10,18,1]{3,0,2,1:T(4,128)S(1)} collective-permute-done((f32[4,10,18,1]{3,0,2,1:T(4,128)S(1)}, f32[4,10,18,1]{3,0,2,1:T(4,128)S(1)}, u32[]{:S(2)}, u32[]{:S(2)}) %collective-permute-start.35) | collective-permute-done | bytes 2912 | tf_op jit(solution)/shard_map/ppermute | solution.py:19
  340.0 1.9 collective-permute-start.36
  341.9 3.8 %collective-permute-start.37 = (f32[4,1,16,128]{3,2,1,0:T(8,128)S(1)}, f32[4,1,16,128]{3,2,1,0:T(8,128)S(1)}, u32[]{:S(2)}, u32[]{:S(2)}) collective-permute-start(f32[4,1,16,128]{3,2,1,0:T(8,128)S(1)} %get-tuple-element.126), channel_id=1, source_target_pairs={{0,8},{8,16},{16,24},{1,9},{9,17},{17,25},{2,10},{10,18},{18,26},{... | collective-permute-start | bytes 98312 | tf_op jit(solution)/shard_map/ppermute | solution.py:19
  346.8 1.6 collective-permute-start.39
  350.7 3.0 collective-permute-done.38
  353.9 1.9 collective-permute-start.40
  359.3 4.7 %collective-permute-done.40 = f32[4,10,18,1]{3,0,2,1:T(4,128)S(1)} collective-permute-done((f32[4,10,18,1]{3,0,2,1:T(4,128)S(1)}, f32[4,10,18,1]{3,0,2,1:T(4,128)S(1)}, u32[]{:S(2)}, u32[]{:S(2)}) %collective-permute-start.40) | collective-permute-done | bytes 2912 | tf_op jit(solution)/shard_map/ppermute | solution.py:20
  364.0 4.4 %collective-permute-done.41 = f32[4,10,18,1]{3,0,2,1:T(4,128)S(1)} collective-permute-done((f32[4,10,18,1]{3,0,2,1:T(4,128)S(1)}, f32[4,10,18,1]{3,0,2,1:T(4,128)S(1)}, u32[]{:S(2)}, u32[]{:S(2)}) %collective-permute-start.41) | collective-permute-done | bytes 2912 | tf_op jit(solution)/shard_map/ppermute | solution.py:19
  (237 shorter events, 42.6 us)
Async XLA Ops:
  0.6 18.4 %copy-start.1 = (f32[8,16,128]{2,1,0:T(8,128)S(1)}, f32[8,16,128]{2,1,0:T(8,128)}, u32[]{:S(2)}) copy-start(f32[8,16,128]{2,1,0:T(8,128)} %param.15) | copy-start | bytes 196612
  1.6 5.6 %collective-permute-start = (f32[5,2,16,128]{3,2,1,0:T(8,128)S(1)}, f32[5,2,16,128]{3,2,1,0:T(8,128)S(1)}, u32[]{:S(2)}, u32[]{:S(2)}) collective-permute-start(f32[5,2,16,128]{3,2,1,0:T(8,128)S(1)} %get-tuple-element.122), channel_id=1, source_target_pairs={{0,8},{8,16},{16,24},{1,9},{9,17},{17,25},{2,10},{10,18},{18,26},{... | collective-permute-start | bytes 245768 | tf_op jit(solution)/shard_map/ppermute | solution.py:19
  5.3 5.8 %collective-permute-start.1 = (f32[5,2,16,128]{3,2,1,0:T(8,128)S(1)}, f32[5,2,16,128]{3,2,1,0:T(8,128)S(1)}, u32[]{:S(2)}, u32[]{:S(2)}) collective-permute-start(f32[5,2,16,128]{3,2,1,0:T(8,128)S(1)} %get-tuple-element.123), channel_id=1, source_target_pairs={{8,0},{16,8},{24,16},{9,1},{17,9},{25,17},{10,2},{18,10},{26,18},{... | collective-permute-start | bytes 245768 | tf_op jit(solution)/shard_map/ppermute | solution.py:20
  12.1 15.0 %collective-permute-start.2 = (f32[5,12,2,128]{3,2,1,0:T(2,128)S(1)}, f32[5,12,2,128]{3,2,1,0:T(2,128)S(1)}, u32[]{:S(2)}, u32[]{:S(2)}) collective-permute-start(f32[5,12,2,128]{3,2,1,0:T(2,128)S(1)} %get-tuple-element.108), channel_id=1, source_target_pairs={{0,4},{1,5},{2,6},{3,7},{8,12},{9,13},{10,14},{11,15},{16,20},{17,... | collective-permute-start | bytes 184328 | tf_op jit(solution)/shard_map/ppermute | solution.py:19
  15.3 11.9 %collective-permute-start.3 = (f32[5,12,2,128]{3,2,1,0:T(2,128)S(1)}, f32[5,12,2,128]{3,2,1,0:T(2,128)S(1)}, u32[]{:S(2)}, u32[]{:S(2)}) collective-permute-start(f32[5,12,2,128]{3,2,1,0:T(2,128)S(1)} %get-tuple-element.109), channel_id=1, source_target_pairs={{4,0},{5,1},{6,2},{7,3},{12,8},{13,9},{14,10},{15,11},{20,16},{21,... | collective-permute-start | bytes 184328 | tf_op jit(solution)/shard_map/ppermute | solution.py:20
  24.5 2.6 copy-start
  28.0 44.4 %collective-permute-start.4 = (f32[5,12,20,2]{2,3,1,0:T(2,128)S(1)}, f32[5,12,20,2]{2,3,1,0:T(2,128)S(1)}, u32[]{:S(2)}, u32[]{:S(2)}) collective-permute-start(f32[5,12,20,2]{2,3,1,0:T(2,128)S(1)} %copy.773), channel_id=1, source_target_pairs={{0,1},{1,2},{2,3},{4,5},{5,6},{6,7},{8,9},{9,10},{10,11},{12,13},{... | collective-permute-start | bytes 28808 | tf_op jit(solution)/shard_map/ppermute | solution.py:19
  29.8 43.1 %collective-permute-start.5 = (f32[5,12,20,2]{2,3,1,0:T(2,128)S(1)}, f32[5,12,20,2]{2,3,1,0:T(2,128)S(1)}, u32[]{:S(2)}, u32[]{:S(2)}) collective-permute-start(f32[5,12,20,2]{2,3,1,0:T(2,128)S(1)} %copy.774), channel_id=1, source_target_pairs={{1,0},{2,1},{3,2},{5,4},{6,5},{7,6},{9,8},{10,9},{11,10},{13,12},{... | collective-permute-start | bytes 28808 | tf_op jit(solution)/shard_map/ppermute | solution.py:20
  90.4 7.9 %copy-start.5 = (f32[4,8,16,128]{3,2,1,0:T(8,128)S(1)}, f32[4,8,16,128]{3,2,1,0:T(8,128)}, u32[]{:S(2)}) copy-start(f32[4,8,16,128]{3,2,1,0:T(8,128)} %param.13) | copy-start | bytes 786436
  90.4 7.9 %copy-start.6 = (f32[4,8,16,128]{3,2,1,0:T(8,128)S(1)}, f32[4,8,16,128]{3,2,1,0:T(8,128)}, u32[]{:S(2)}) copy-start(f32[4,8,16,128]{3,2,1,0:T(8,128)} %param.12) | copy-start | bytes 786436
  90.8 8.9 %collective-permute-start.6 = (f32[5,2,8,64]{3,2,1,0:T(8,128)S(1)}, f32[5,2,8,64]{3,2,1,0:T(8,128)S(1)}, u32[]{:S(2)}, u32[]{:S(2)}) collective-permute-start(f32[5,2,8,64]{3,2,1,0:T(8,128)S(1)} %get-tuple-element.154), channel_id=1, source_target_pairs={{0,8},{8,16},{16,24},{1,9},{9,17},{17,25},{2,10},{10,18},{18,26},{... | collective-permute-start | bytes 61448 | tf_op jit(solution)/shard_map/ppermute | solution.py:19
  96.1 5.3 %collective-permute-start.7 = (f32[5,2,8,64]{3,2,1,0:T(8,128)S(1)}, f32[5,2,8,64]{3,2,1,0:T(8,128)S(1)}, u32[]{:S(2)}, u32[]{:S(2)}) collective-permute-start(f32[5,2,8,64]{3,2,1,0:T(8,128)S(1)} %get-tuple-element.155), channel_id=1, source_target_pairs={{8,0},{16,8},{24,16},{9,1},{17,9},{25,17},{10,2},{18,10},{26,18},{... | collective-permute-start | bytes 61448 | tf_op jit(solution)/shard_map/ppermute | solution.py:20
  99.0 14.4 %copy-start.2 = (f32[4,8,16,128]{3,0,2,1:T(4,128)}, f32[4,8,16,128]{3,0,2,1:T(4,128)S(1)}, u32[]{:S(2)}) copy-start(f32[4,8,16,128]{3,0,2,1:T(4,128)S(1)} %convolution_subtract_fusion) | copy-start | bytes 786436
  101.5 3.1 collective-permute-start.8
  103.2 4.7 %collective-permute-start.9 = (f32[5,8,2,64]{3,1,2,0:T(8,128)S(1)}, f32[5,8,2,64]{3,1,2,0:T(8,128)S(1)}, u32[]{:S(2)}, u32[]{:S(2)}) collective-permute-start(f32[5,8,2,64]{3,1,2,0:T(8,128)S(1)} %copy.846), channel_id=1, source_target_pairs={{4,0},{5,1},{6,2},{7,3},{12,8},{13,9},{14,10},{15,11},{20,16},{21,... | collective-permute-start | bytes 61448 | tf_op jit(solution)/shard_map/ppermute | solution.py:20
  108.1 9.3 %collective-permute-start.10 = (f32[5,8,12,2]{3,1,2,0:T(8,128)S(1)}, f32[5,8,12,2]{3,1,2,0:T(8,128)S(1)}, u32[]{:S(2)}, u32[]{:S(2)}) collective-permute-start(f32[5,8,12,2]{3,1,2,0:T(8,128)S(1)} %get-tuple-element.130), channel_id=1, source_target_pairs={{0,1},{1,2},{2,3},{4,5},{5,6},{6,7},{8,9},{9,10},{10,11},{12,13},{... | collective-permute-start | bytes 11528 | tf_op jit(solution)/shard_map/ppermute | solution.py:19
  109.4 9.7 %collective-permute-start.11 = (f32[5,8,12,2]{3,1,2,0:T(8,128)S(1)}, f32[5,8,12,2]{3,1,2,0:T(8,128)S(1)}, u32[]{:S(2)}, u32[]{:S(2)}) collective-permute-start(f32[5,8,12,2]{3,1,2,0:T(8,128)S(1)} %get-tuple-element.131), channel_id=1, source_target_pairs={{1,0},{2,1},{3,2},{5,4},{6,5},{7,6},{9,8},{10,9},{11,10},{13,12},{... | collective-permute-start | bytes 11528 | tf_op jit(solution)/shard_map/ppermute | solution.py:20
  121.7 42.9 %collective-permute-start.12 = (f32[5,2,4,32]{3,2,1,0:T(4,128)S(1)}, f32[5,2,4,32]{3,2,1,0:T(4,128)S(1)}, u32[]{:S(2)}, u32[]{:S(2)}) collective-permute-start(f32[5,2,4,32]{3,2,1,0:T(4,128)S(1)} %pad_maximum_fusion.50), channel_id=1, source_target_pairs={{0,8},{8,16},{16,24},{1,9},{9,17},{17,25},{2,10},{10,18},{18,26},{... | collective-permute-start | bytes 15368 | tf_op jit(solution)/shard_map/ppermute | solution.py:19
  123.6 41.0 %collective-permute-start.13 = (f32[5,2,4,32]{3,2,1,0:T(4,128)S(1)}, f32[5,2,4,32]{3,2,1,0:T(4,128)S(1)}, u32[]{:S(2)}, u32[]{:S(2)}) collective-permute-start(f32[5,2,4,32]{3,2,1,0:T(4,128)S(1)} %pad_maximum_fusion.50), channel_id=1, source_target_pairs={{8,0},{16,8},{24,16},{9,1},{17,9},{25,17},{10,2},{18,10},{26,18},{... | collective-permute-start | bytes 15368 | tf_op jit(solution)/shard_map/ppermute | solution.py:20
  164.7 5.8 %collective-permute-start.14 = (f32[5,6,2,32]{3,2,1,0:T(2,128)S(1)}, f32[5,6,2,32]{3,2,1,0:T(2,128)S(1)}, u32[]{:S(2)}, u32[]{:S(2)}) collective-permute-start(f32[5,6,2,32]{3,2,1,0:T(2,128)S(1)} %get-tuple-element.158), channel_id=1, source_target_pairs={{0,4},{1,5},{2,6},{3,7},{8,12},{9,13},{10,14},{11,15},{16,20},{17,... | collective-permute-start | bytes 23048 | tf_op jit(solution)/shard_map/ppermute | solution.py:19
  169.0 4.6 %collective-permute-start.15 = (f32[5,6,2,32]{3,2,1,0:T(2,128)S(1)}, f32[5,6,2,32]{3,2,1,0:T(2,128)S(1)}, u32[]{:S(2)}, u32[]{:S(2)}) collective-permute-start(f32[5,6,2,32]{3,2,1,0:T(2,128)S(1)} %get-tuple-element.159), channel_id=1, source_target_pairs={{4,0},{5,1},{6,2},{7,3},{12,8},{13,9},{14,10},{15,11},{20,16},{21,... | collective-permute-start | bytes 23048 | tf_op jit(solution)/shard_map/ppermute | solution.py:20
  173.8 5.6 %collective-permute-start.16 = (f32[5,6,8,2]{3,2,1,0:T(8,128)S(1)}, f32[5,6,8,2]{3,2,1,0:T(8,128)S(1)}, u32[]{:S(2)}, u32[]{:S(2)}) collective-permute-start(f32[5,6,8,2]{3,2,1,0:T(8,128)S(1)} %get-tuple-element.150), channel_id=1, source_target_pairs={{0,1},{1,2},{2,3},{4,5},{5,6},{6,7},{8,9},{9,10},{10,11},{12,13},{... | collective-permute-start | bytes 5768 | tf_op jit(solution)/shard_map/ppermute | solution.py:19
  175.1 5.8 %collective-permute-start.17 = (f32[5,6,8,2]{3,2,1,0:T(8,128)S(1)}, f32[5,6,8,2]{3,2,1,0:T(8,128)S(1)}, u32[]{:S(2)}, u32[]{:S(2)}) collective-permute-start(f32[5,6,8,2]{3,2,1,0:T(8,128)S(1)} %get-tuple-element.151), channel_id=1, source_target_pairs={{1,0},{2,1},{3,2},{5,4},{6,5},{7,6},{9,8},{10,9},{11,10},{13,12},{... | collective-permute-start | bytes 5768 | tf_op jit(solution)/shard_map/ppermute | solution.py:20
  247.1 12.6 %collective-permute-start.18 = (f32[4,1,4,32]{3,2,1,0:T(4,128)S(1)}, f32[4,1,4,32]{3,2,1,0:T(4,128)S(1)}, u32[]{:S(2)}, u32[]{:S(2)}) collective-permute-start(f32[4,1,4,32]{3,2,1,0:T(4,128)S(1)} %get-tuple-element.175), channel_id=1, source_target_pairs={{8,0},{16,8},{24,16},{9,1},{17,9},{25,17},{10,2},{18,10},{26,18},{... | collective-permute-start | bytes 6152 | tf_op jit(solution)/shard_map/ppermute | solution.py:20
  255.7 4.3 %collective-permute-start.19 = (f32[4,1,4,32]{3,2,1,0:T(4,128)S(1)}, f32[4,1,4,32]{3,2,1,0:T(4,128)S(1)}, u32[]{:S(2)}, u32[]{:S(2)}) collective-permute-start(f32[4,1,4,32]{3,2,1,0:T(4,128)S(1)} %get-tuple-element.174), channel_id=1, source_target_pairs={{0,8},{8,16},{16,24},{1,9},{9,17},{17,25},{2,10},{10,18},{18,26},{... | collective-permute-start | bytes 6152 | tf_op jit(solution)/shard_map/ppermute | solution.py:19
  260.1 4.6 %collective-permute-start.21 = (f32[4,4,1,32]{3,2,1,0:T(1,128)S(1)}, f32[4,4,1,32]{3,2,1,0:T(1,128)S(1)}, u32[]{:S(2)}, u32[]{:S(2)}) collective-permute-start(f32[4,4,1,32]{3,2,1,0:T(1,128)S(1)} %get-tuple-element.167), channel_id=1, source_target_pairs={{0,4},{1,5},{2,6},{3,7},{8,12},{9,13},{10,14},{11,15},{16,20},{17,... | collective-permute-start | bytes 6152 | tf_op jit(solution)/shard_map/ppermute | solution.py:19
  263.3 4.4 %collective-permute-start.20 = (f32[4,4,1,32]{3,2,1,0:T(1,128)S(1)}, f32[4,4,1,32]{3,2,1,0:T(1,128)S(1)}, u32[]{:S(2)}, u32[]{:S(2)}) collective-permute-start(f32[4,4,1,32]{3,2,1,0:T(1,128)S(1)} %get-tuple-element.166), channel_id=1, source_target_pairs={{4,0},{5,1},{6,2},{7,3},{12,8},{13,9},{14,10},{15,11},{20,16},{21,... | collective-permute-start | bytes 6152 | tf_op jit(solution)/shard_map/ppermute | solution.py:20
  267.8 3.6 collective-permute-start.22
  269.5 6.2 %collective-permute-start.23 = (f32[4,4,6,1]{3,1,2,0:T(4,128)S(1)}, f32[4,4,6,1]{3,1,2,0:T(4,128)S(1)}, u32[]{:S(2)}, u32[]{:S(2)}) collective-permute-start(f32[4,4,6,1]{3,1,2,0:T(4,128)S(1)} %get-tuple-element.163), channel_id=1, source_target_pairs={{0,1},{1,2},{2,3},{4,5},{5,6},{6,7},{8,9},{9,10},{10,11},{12,13},{... | collective-permute-start | bytes 1160 | tf_op jit(solution)/shard_map/ppermute | solution.py:19
  276.6 8.8 %collective-permute-start.24 = (f32[4,1,8,64]{3,2,1,0:T(8,128)S(1)}, f32[4,1,8,64]{3,2,1,0:T(8,128)S(1)}, u32[]{:S(2)}, u32[]{:S(2)}) collective-permute-start(f32[4,1,8,64]{3,2,1,0:T(8,128)S(1)} %get-tuple-element.157), channel_id=1, source_target_pairs={{8,0},{16,8},{24,16},{9,1},{17,9},{25,17},{10,2},{18,10},{26,18},{... | collective-permute-start | bytes 24584 | tf_op jit(solution)/shard_map/ppermute | solution.py:20
  279.4 6.1 %collective-permute-start.25 = (f32[4,1,8,64]{3,2,1,0:T(8,128)S(1)}, f32[4,1,8,64]{3,2,1,0:T(8,128)S(1)}, u32[]{:S(2)}, u32[]{:S(2)}) collective-permute-start(f32[4,1,8,64]{3,2,1,0:T(8,128)S(1)} %get-tuple-element.156), channel_id=1, source_target_pairs={{0,8},{8,16},{16,24},{1,9},{9,17},{17,25},{2,10},{10,18},{18,26},{... | collective-permute-start | bytes 24584 | tf_op jit(solution)/shard_map/ppermute | solution.py:19
  285.6 3.3 collective-permute-start.27
  287.6 4.4 %collective-permute-start.26 = (f32[4,6,1,64]{3,0,2,1:T(4,128)S(1)}, f32[4,6,1,64]{3,0,2,1:T(4,128)S(1)}, u32[]{:S(2)}, u32[]{:S(2)}) collective-permute-start(f32[4,6,1,64]{3,0,2,1:T(4,128)S(1)} %copy.737), channel_id=1, source_target_pairs={{4,0},{5,1},{6,2},{7,3},{12,8},{13,9},{14,10},{15,11},{20,16},{21,... | collective-permute-start | bytes 18440 | tf_op jit(solution)/shard_map/ppermute | solution.py:20
  292.2 5.8 %collective-permute-start.28 = (f32[4,6,10,1]{3,0,2,1:T(4,128)S(1)}, f32[4,6,10,1]{3,0,2,1:T(4,128)S(1)}, u32[]{:S(2)}, u32[]{:S(2)}) collective-permute-start(f32[4,6,10,1]{3,0,2,1:T(4,128)S(1)} %get-tuple-element.146), channel_id=1, source_target_pairs={{1,0},{2,1},{3,2},{5,4},{6,5},{7,6},{9,8},{10,9},{11,10},{13,12},{... | collective-permute-start | bytes 2888 | tf_op jit(solution)/shard_map/ppermute | solution.py:20
  295.9 6.2 %collective-permute-start.29 = (f32[4,6,10,1]{3,0,2,1:T(4,128)S(1)}, f32[4,6,10,1]{3,0,2,1:T(4,128)S(1)}, u32[]{:S(2)}, u32[]{:S(2)}) collective-permute-start(f32[4,6,10,1]{3,0,2,1:T(4,128)S(1)} %get-tuple-element.147), channel_id=1, source_target_pairs={{0,1},{1,2},{2,3},{4,5},{5,6},{6,7},{8,9},{9,10},{10,11},{12,13},{... | collective-permute-start | bytes 2888 | tf_op jit(solution)/shard_map/ppermute | solution.py:19
  307.6 10.6 %collective-permute-start.30 = (f32[4,1,16,128]{3,2,1,0:T(8,128)S(1)}, f32[4,1,16,128]{3,2,1,0:T(8,128)S(1)}, u32[]{:S(2)}, u32[]{:S(2)}) collective-permute-start(f32[4,1,16,128]{3,2,1,0:T(8,128)S(1)} %get-tuple-element.129), channel_id=1, source_target_pairs={{8,0},{16,8},{24,16},{9,1},{17,9},{25,17},{10,2},{18,10},{26,18},{... | collective-permute-start | bytes 98312 | tf_op jit(solution)/shard_map/ppermute | solution.py:20
  309.5 8.7 %collective-permute-start.31 = (f32[4,1,16,128]{3,2,1,0:T(8,128)S(1)}, f32[4,1,16,128]{3,2,1,0:T(8,128)S(1)}, u32[]{:S(2)}, u32[]{:S(2)}) collective-permute-start(f32[4,1,16,128]{3,2,1,0:T(8,128)S(1)} %get-tuple-element.128), channel_id=1, source_target_pairs={{0,8},{8,16},{16,24},{1,9},{9,17},{17,25},{2,10},{10,18},{18,26},{... | collective-permute-start | bytes 98312 | tf_op jit(solution)/shard_map/ppermute | solution.py:19
  318.3 3.5 collective-permute-start.33
  320.5 4.5 %collective-permute-start.32 = (f32[4,10,1,128]{3,0,2,1:T(4,128)S(1)}, f32[4,10,1,128]{3,0,2,1:T(4,128)S(1)}, u32[]{:S(2)}, u32[]{:S(2)}) collective-permute-start(f32[4,10,1,128]{3,0,2,1:T(4,128)S(1)} %copy.747), channel_id=1, source_target_pairs={{4,0},{5,1},{6,2},{7,3},{12,8},{13,9},{14,10},{15,11},{20,16},{21,... | collective-permute-start | bytes 61448 | tf_op jit(solution)/shard_map/ppermute | solution.py:20
  325.3 9.9 %collective-permute-start.34 = (f32[4,10,18,1]{3,0,2,1:T(4,128)S(1)}, f32[4,10,18,1]{3,0,2,1:T(4,128)S(1)}, u32[]{:S(2)}, u32[]{:S(2)}) collective-permute-start(f32[4,10,18,1]{3,0,2,1:T(4,128)S(1)} %get-tuple-element.116), channel_id=1, source_target_pairs={{1,0},{2,1},{3,2},{5,4},{6,5},{7,6},{9,8},{10,9},{11,10},{13,12},{... | collective-permute-start | bytes 8648 | tf_op jit(solution)/shard_map/ppermute | solution.py:20
  328.9 10.3 %collective-permute-start.35 = (f32[4,10,18,1]{3,0,2,1:T(4,128)S(1)}, f32[4,10,18,1]{3,0,2,1:T(4,128)S(1)}, u32[]{:S(2)}, u32[]{:S(2)}) collective-permute-start(f32[4,10,18,1]{3,0,2,1:T(4,128)S(1)} %get-tuple-element.117), channel_id=1, source_target_pairs={{0,1},{1,2},{2,3},{4,5},{5,6},{6,7},{8,9},{9,10},{10,11},{12,13},{... | collective-permute-start | bytes 8648 | tf_op jit(solution)/shard_map/ppermute | solution.py:19
  331.1 14.6 %copy-start.3 = (f32[4,8,16,128]{3,0,2,1:T(4,128)S(1)}, f32[4,8,16,128]{3,0,2,1:T(4,128)}, u32[]{:S(2)}) copy-start(f32[4,8,16,128]{3,0,2,1:T(4,128)} %copy-done.2) | copy-start | bytes 786436
  339.9 28.9 %copy-start.4 = (f32[4,8,16,128]{3,2,1,0:T(8,128)}, f32[4,8,16,128]{3,2,1,0:T(8,128)S(1)}, u32[]{:S(2)}) copy-start(f32[4,8,16,128]{3,2,1,0:T(8,128)S(1)} %fusion.30) | copy-start | bytes 786436
  340.0 6.4 %collective-permute-start.36 = (f32[4,1,16,128]{3,2,1,0:T(8,128)S(1)}, f32[4,1,16,128]{3,2,1,0:T(8,128)S(1)}, u32[]{:S(2)}, u32[]{:S(2)}) collective-permute-start(f32[4,1,16,128]{3,2,1,0:T(8,128)S(1)} %get-tuple-element.127), channel_id=1, source_target_pairs={{8,0},{16,8},{24,16},{9,1},{17,9},{25,17},{10,2},{18,10},{26,18},{... | collective-permute-start | bytes 98312 | tf_op jit(solution)/shard_map/ppermute | solution.py:20
  341.9 4.9 %collective-permute-start.37 = (f32[4,1,16,128]{3,2,1,0:T(8,128)S(1)}, f32[4,1,16,128]{3,2,1,0:T(8,128)S(1)}, u32[]{:S(2)}, u32[]{:S(2)}) collective-permute-start(f32[4,1,16,128]{3,2,1,0:T(8,128)S(1)} %get-tuple-element.126), channel_id=1, source_target_pairs={{0,8},{8,16},{16,24},{1,9},{9,17},{17,25},{2,10},{10,18},{18,26},{... | collective-permute-start | bytes 98312 | tf_op jit(solution)/shard_map/ppermute | solution.py:19
  346.8 3.6 collective-permute-start.39
  349.2 4.5 %collective-permute-start.38 = (f32[4,10,1,128]{3,0,2,1:T(4,128)S(1)}, f32[4,10,1,128]{3,0,2,1:T(4,128)S(1)}, u32[]{:S(2)}, u32[]{:S(2)}) collective-permute-start(f32[4,10,1,128]{3,0,2,1:T(4,128)S(1)} %copy.754), channel_id=1, source_target_pairs={{4,0},{5,1},{6,2},{7,3},{12,8},{13,9},{14,10},{15,11},{20,16},{21,... | collective-permute-start | bytes 61448 | tf_op jit(solution)/shard_map/ppermute | solution.py:20
  353.9 10.0 %collective-permute-start.40 = (f32[4,10,18,1]{3,0,2,1:T(4,128)S(1)}, f32[4,10,18,1]{3,0,2,1:T(4,128)S(1)}, u32[]{:S(2)}, u32[]{:S(2)}) collective-permute-start(f32[4,10,18,1]{3,0,2,1:T(4,128)S(1)} %get-tuple-element.112), channel_id=1, source_target_pairs={{1,0},{2,1},{3,2},{5,4},{6,5},{7,6},{9,8},{10,9},{11,10},{13,12},{... | collective-permute-start | bytes 8648 | tf_op jit(solution)/shard_map/ppermute | solution.py:20
  355.9 12.5 %collective-permute-start.41 = (f32[4,10,18,1]{3,0,2,1:T(4,128)S(1)}, f32[4,10,18,1]{3,0,2,1:T(4,128)S(1)}, u32[]{:S(2)}, u32[]{:S(2)}) collective-permute-start(f32[4,10,18,1]{3,0,2,1:T(4,128)S(1)} %get-tuple-element.113), channel_id=1, source_target_pairs={{0,1},{1,2},{2,3},{4,5},{5,6},{6,7},{8,9},{9,10},{10,11},{12,13},{... | collective-permute-start | bytes 8648 | tf_op jit(solution)/shard_map/ppermute | solution.py:19
